TPU v7x, 32 devices: a whole 2x2x4 slice. The times are simulated.
32 devices in a mesh: cond: 2 (over x), gx: 4 (over y, core), yz: 4 (over z).
Axes of the slice: x: 2, y: 2, z: 4, core: 2. Of those that a mesh axis runs over, the one named last changes fastest.
Arguments:
- adjoint: float32 [2, 5, 32, 64, 256], P('cond', None, 'gx', 'yz'), may hold values from -6 to 6
- objective_gradient: float32 [2, 5, 32, 64, 256], P('cond', None, 'gx', 'yz'), may hold values from -6 to 6
- diagonal: float32 [32, 64, 256], P('gx', 'yz'), may hold values from 4 to 12
- flux_blocks: float32 [2, 6, 5, 5], P('cond'), may hold values from -1 to 1
- flux_sensitivity: bfloat16 [2, 5, 32, 64, 256], P('cond', None, 'gx', 'yz'), may hold values from -6 to 6
- surface_mask: int32 [32, 64, 256], P('gx', 'yz'), may hold values 0 or 1
- patch_band_slot: int32 [32, 64], P('gx', 'yz'), may hold values from 0 to 62
- design_basis: float32 [256, 128], replicated, may hold values from -0.046875 to 0.046875
- condition_weights: int32 [2], replicated, may hold values from 1 to 999, as said below
Outputs:
- smoothed: float32 [2, 5, 32, 64, 256], P('cond', None, 'gx', 'yz')
- residual: float32 [2, 5, 32, 64, 256], P('cond', None, 'gx', 'yz')
- design_gradient: float32 [4096], P(('gx', 'yz'))
Inputs may be any that keep to these rules, and one draw needn't show every extreme that they name: `condition_weights`: positive integer weights; one condition has weight 999.
All inputs are finite; a program needn't handle non-finite values. No bound on the sum of `surface_mask` on one device may be relied on, other than what follows from the above.
Results may differ from a plain program's by a relative error of at most 0.0003.
Values sent between devices are 32-bit elements; how exact they have to be, the bound alone decides.
A program may use at most 64 MiB of HBM per device.

v0:
```python
import jax
import jax.numpy as jnp
from jax import lax
from jax.sharding import PartitionSpec as P

NDES = 4096
relaxation = 0.8
neighbour_starts = ((2, 1, 1), (0, 1, 1), (1, 2, 1), (1, 0, 1), (1, 1, 2), (1, 1, 0))


def with_halo(block, sides, width):
    for axis, dim in sides:
        count = lax.axis_size(axis)
        forward = [(i, i + 1) for i in range(count - 1)]
        backward = [(target, source) for source, target in forward]
        low = lax.ppermute(
            lax.slice_in_dim(block, block.shape[dim] - width, None, axis=dim), axis, forward
        )
        high = lax.ppermute(lax.slice_in_dim(block, 0, width, axis=dim), axis, backward)
        block = jnp.concatenate([low, block, high], axis=dim)
    return block


def apply_operator(padded_field, diagonal, blocks):
    size_x = padded_field.shape[1] - 2
    size_y = padded_field.shape[2] - 2
    size_z = padded_field.shape[3] - 2
    result = diagonal * padded_field[:, 1:-1, 1:-1, 1:-1]
    for direction in range(6):
        start_x, start_y, start_z = neighbour_starts[direction]
        shifted = padded_field[
            :, start_x : start_x + size_x, start_y : start_y + size_y, start_z : start_z + size_z
        ]
        result = result - jnp.einsum(
            "ec,exyz->cxyz", blocks[direction], shifted, precision=lax.Precision.HIGHEST
        )
    return result


def spread_bands(slot_lookup):
    halfway = slot_lookup.shape[1] // 2
    first_half = jnp.pad(slot_lookup[:, :halfway], ((0, 1), (0, 0)))
    second_half = jnp.pad(slot_lookup[:, halfway:], ((1, 0), (0, 0)))
    return (first_half + second_half).reshape(-1)


def pad_third(values):
    return jnp.pad(values, ((0, 0), (0, 0), (0, 0), (1, 1)))


def local(
    adjoint,
    objective_gradient,
    diagonal,
    flux_blocks,
    flux_sensitivity,
    surface_mask,
    patch_band_slot,
    design_basis,
    condition_weights,
):
    blocks = flux_blocks[0]
    source = objective_gradient[0]
    start_field = adjoint[0]

    def operate(values):
        haloed = with_halo(values, (("gx", 1), ("yz", 2)), 1)
        return apply_operator(pad_third(haloed), diagonal, blocks)

    relaxed = start_field + relaxation * (source - operate(start_field)) / diagonal
    smoothed = relaxed + relaxation * (source - operate(relaxed)) / diagonal
    residual = source - operate(smoothed)
    surface = surface_mask.astype(jnp.float32) * jnp.sum(
        smoothed * flux_sensitivity[0].astype(jnp.float32), axis=0
    )
    projected_gradient = jnp.dot(
        surface.reshape(-1, surface.shape[-1]),
        design_basis,
        precision=lax.Precision.HIGHEST,
        preferred_element_type=jnp.float32,
    )
    slot_count = 2 * NDES // design_basis.shape[1] - 1
    onehot = (jnp.arange(slot_count)[:, None] == patch_band_slot.reshape(1, -1)).astype(jnp.float32)
    slot_lookup = jnp.dot(
        onehot,
        projected_gradient,
        precision=lax.Precision.HIGHEST,
        preferred_element_type=jnp.float32,
    )
    gradient = spread_bands(slot_lookup)
    weights_float = condition_weights.astype(jnp.float32)
    picked = jnp.arange(weights_float.shape[0]) == lax.axis_index("cond")
    local_portion = jnp.sum(jnp.where(picked, weights_float, 0.0)) / jnp.sum(weights_float)
    summed = lax.psum(local_portion * gradient, ("cond", "gx", "yz"))
    pieces = NDES // lax.axis_size(("gx", "yz"))
    design_gradient = lax.dynamic_slice_in_dim(
        summed, lax.axis_index(("gx", "yz")) * pieces, pieces, 0
    )
    return (smoothed[None], residual[None], design_gradient)


def solution(mesh):
    placed = (
        P("cond", None, "gx", "yz", None),
        P("cond", None, "gx", "yz", None),
        P("gx", "yz", None),
        P("cond", None, None, None),
        P("cond", None, "gx", "yz", None),
        P("gx", "yz", None),
        P("gx", "yz"),
        P(),
        P(),
    )
    return jax.shard_map(
        local,
        mesh=mesh,
        in_specs=placed,
        out_specs=(
            P("cond", None, "gx", "yz", None),
            P("cond", None, "gx", "yz", None),
            P(("gx", "yz")),
        ),
        check_vma=False,
    )
```

profile of v0, /device:TPU:12, one launch (start us, length us, event | category | flops | bytes accessed | tf_op | source)
XLA Modules:
  0.0 115.4 jit_solution(11190379338171602337)
XLA Ops:
  0.6 0.0 copy-start
  0.7 1.5 %copy.88 = f32[1,5,8,16,256]{4,1,3,2,0:T(8,128)S(1)} copy(f32[1,5,8,16,256]{4,3,2,1,0:T(8,128)} %param.9) | data formatting | bytes 1310720 | tf_op args[0]
  2.2 1.9 %collective-permute-start = (f32[5,1,16,256]{3,0,2,1:T(8,128)S(1)}, f32[5,1,16,256]{3,0,2,1:T(8,128)S(1)}, u32[]{:S(2)}, u32[]{:S(2)}) collective-permute-start(f32[5,1,16,256]{3,0,2,1:T(8,128)S(1)} %get-tuple-element.19), channel_id=1, source_target_pairs={{4,0},{8,4},{12,8},{5,1},{9,5},{13,9},{6,2},{10,6},{14,10},{7,3},{... | collective-permute-start | bytes 245768 | tf_op jit(solution)/shard_map/ppermute | solution.py:19
  4.1 2.4 %collective-permute-start.1 = (f32[5,1,16,256]{3,0,2,1:T(8,128)S(1)}, f32[5,1,16,256]{3,0,2,1:T(8,128)S(1)}, u32[]{:S(2)}, u32[]{:S(2)}) collective-permute-start(f32[5,1,16,256]{3,0,2,1:T(8,128)S(1)} %get-tuple-element.18), channel_id=1, source_target_pairs={{0,4},{4,8},{8,12},{1,5},{5,9},{9,13},{2,6},{6,10},{10,14},{3,7},{... | collective-permute-start | bytes 245768 | tf_op jit(solution)/shard_map/ppermute | solution.py:16
  6.6 0.2 fusion.157
  6.8 0.1 copy.82
  6.9 0.1 copy.81
  7.0 0.1 copy.80
  7.2 0.1 copy.79
  7.3 0.1 copy.78
  7.4 0.1 copy.77
  7.6 0.1 eq.24
  7.6 0.0 collective-permute-done
  7.7 2.8 %collective-permute-done.1 = f32[5,1,16,256]{3,0,2,1:T(8,128)S(1)} collective-permute-done((f32[5,1,16,256]{3,0,2,1:T(8,128)S(1)}, f32[5,1,16,256]{3,0,2,1:T(8,128)S(1)}, u32[]{:S(2)}, u32[]{:S(2)}) %collective-permute-start.1) | collective-permute-done | bytes 81952 | tf_op jit(solution)/shard_map/ppermute | solution.py:16
  10.4 2.4 %collective-permute-start.2 = (f32[5,10,1,256]{3,0,2,1:T(8,128)S(1)}, f32[5,10,1,256]{3,0,2,1:T(8,128)S(1)}, u32[]{:S(2)}, u32[]{:S(2)}) collective-permute-start(f32[5,10,1,256]{3,0,2,1:T(8,128)S(1)} %get-tuple-element.13), channel_id=1, source_target_pairs={{1,0},{2,1},{3,2},{5,4},{6,5},{7,6},{9,8},{10,9},{11,10},{13,12},{... | collective-permute-start | bytes 153608 | tf_op jit(solution)/shard_map/ppermute | solution.py:19
  12.8 3.5 %collective-permute-start.3 = (f32[5,10,1,256]{3,0,2,1:T(8,128)S(1)}, f32[5,10,1,256]{3,0,2,1:T(8,128)S(1)}, u32[]{:S(2)}, u32[]{:S(2)}) collective-permute-start(f32[5,10,1,256]{3,0,2,1:T(8,128)S(1)} %get-tuple-element.12), channel_id=1, source_target_pairs={{0,1},{1,2},{2,3},{4,5},{5,6},{6,7},{8,9},{9,10},{10,11},{12,13},{... | collective-permute-start | bytes 153608 | tf_op jit(solution)/shard_map/ppermute | solution.py:16
  16.3 1.1 convolution_bitcast_fusion.4
  17.4 0.0 collective-permute-done.2
  17.4 1.8 %collective-permute-done.3 = f32[5,10,1,256]{3,0,2,1:T(8,128)S(1)} collective-permute-done((f32[5,10,1,256]{3,0,2,1:T(8,128)S(1)}, f32[5,10,1,256]{3,0,2,1:T(8,128)S(1)}, u32[]{:S(2)}, u32[]{:S(2)}) %collective-permute-start.3) | collective-permute-done | bytes 51232 | tf_op jit(solution)/shard_map/ppermute | solution.py:16
  19.1 0.6 select_maximum_fusion.8
  19.8 1.0 convolution_bitcast_fusion.10
  20.9 1.2 %convolution_bitcast_fusion.11 = f32[5,8,16,256]{3,0,2,1:T(8,128)S(1)} fusion(f32[5,10,18,258]{3,0,2,1:T(8,128)S(1)} %select_maximum_fusion.8, f32[1,1,5,5]{3,2,1,0:T(8,128)S(1)} %copy.81), kind=kOutput, calls=%fused_computation.86 | convolution fusion | flops 9830400 | bytes 1708032 | tf_op jit(solution)/shard_map/ec,exyz->cxyz/dot_general | solution.py:34
  22.1 0.0 copy-start.1
  22.1 0.0 copy-start.2
  22.1 1.1 fusion.61
  23.2 1.1 fusion.64
  24.3 0.0 copy-start.7
  24.3 2.0 %fusion.94 = f32[5,8,16,256]{3,0,2,1:T(8,128)S(1)} fusion(f32[5,8,16,256]{3,0,2,1:T(8,128)S(1)} %bitcast.184, f32[5,8,16,256]{3,0,2,1:T(8,128)S(1)} %convolution_bitcast_fusion.10, f32[5,8,16,256]{3,0,2,1:T(8,128)S(1)} %convolution_bitcast_fusion.11, f32[5,8,16,256]{3,0,2,1:T(8,128)S(1)} %fusion.61, f32[5,8,16,256]{3,0,2,1:T(8,128)S(1)} %fusion.64, ...), kind=kOutput, calls=%fused_computation.108 | convolution fusion | flops 11816960 | bytes 5455972 | tf_op jit(solution)/shard_map/ec,exyz->cxyz/dot_general | solution.py:34
  26.3 1.9 %collective-permute-start.4 = (f32[5,1,16,256]{3,0,2,1:T(8,128)S(1)}, f32[5,1,16,256]{3,0,2,1:T(8,128)S(1)}, u32[]{:S(2)}, u32[]{:S(2)}) collective-permute-start(f32[5,1,16,256]{3,0,2,1:T(8,128)S(1)} %get-tuple-element.17), channel_id=1, source_target_pairs={{4,0},{8,4},{12,8},{5,1},{9,5},{13,9},{6,2},{10,6},{14,10},{7,3},{... | collective-permute-start | bytes 245768 | tf_op jit(solution)/shard_map/ppermute | solution.py:19
  28.3 2.4 %collective-permute-start.5 = (f32[5,1,16,256]{3,0,2,1:T(8,128)S(1)}, f32[5,1,16,256]{3,0,2,1:T(8,128)S(1)}, u32[]{:S(2)}, u32[]{:S(2)}) collective-permute-start(f32[5,1,16,256]{3,0,2,1:T(8,128)S(1)} %get-tuple-element.16), channel_id=1, source_target_pairs={{0,4},{4,8},{8,12},{1,5},{5,9},{9,13},{2,6},{6,10},{10,14},{3,7},{... | collective-permute-start | bytes 245768 | tf_op jit(solution)/shard_map/ppermute | solution.py:16
  30.7 0.6 convert_reduce_fusion
  32.7 1.9 %collective-permute-done.5 = f32[5,1,16,256]{3,0,2,1:T(8,128)S(1)} collective-permute-done((f32[5,1,16,256]{3,0,2,1:T(8,128)S(1)}, f32[5,1,16,256]{3,0,2,1:T(8,128)S(1)}, u32[]{:S(2)}, u32[]{:S(2)}) %collective-permute-start.5) | collective-permute-done | bytes 81952 | tf_op jit(solution)/shard_map/ppermute | solution.py:16
  34.6 1.9 %collective-permute-start.6 = (f32[5,10,1,256]{3,0,2,1:T(8,128)S(1)}, f32[5,10,1,256]{3,0,2,1:T(8,128)S(1)}, u32[]{:S(2)}, u32[]{:S(2)}) collective-permute-start(f32[5,10,1,256]{3,0,2,1:T(8,128)S(1)} %get-tuple-element.11), channel_id=1, source_target_pairs={{1,0},{2,1},{3,2},{5,4},{6,5},{7,6},{9,8},{10,9},{11,10},{13,12},{... | collective-permute-start | bytes 153608 | tf_op jit(solution)/shard_map/ppermute | solution.py:19
  36.5 4.1 %collective-permute-start.7 = (f32[5,10,1,256]{3,0,2,1:T(8,128)S(1)}, f32[5,10,1,256]{3,0,2,1:T(8,128)S(1)}, u32[]{:S(2)}, u32[]{:S(2)}) collective-permute-start(f32[5,10,1,256]{3,0,2,1:T(8,128)S(1)} %get-tuple-element.10), channel_id=1, source_target_pairs={{0,1},{1,2},{2,3},{4,5},{5,6},{6,7},{8,9},{9,10},{10,11},{12,13},{... | collective-permute-start | bytes 153608 | tf_op jit(solution)/shard_map/ppermute | solution.py:16
  40.6 1.1 convolution_bitcast_fusion.2
  41.7 1.1 collective-permute-done.7
  42.8 0.6 select_maximum_fusion.4
  43.5 1.0 convolution_bitcast_fusion.8
  44.5 1.2 %convolution_bitcast_fusion.9 = f32[5,8,16,256]{3,0,2,1:T(8,128)S(1)} fusion(f32[5,10,18,258]{3,0,2,1:T(8,128)S(1)} %select_maximum_fusion.4, f32[1,1,5,5]{3,2,1,0:T(8,128)S(1)} %copy.81), kind=kOutput, calls=%fused_computation.84 | convolution fusion | flops 9830400 | bytes 1708032 | tf_op jit(solution)/shard_map/ec,exyz->cxyz/dot_general | solution.py:34
  45.8 0.0 copy-start.3
  45.8 1.1 fusion.55
  46.9 1.1 fusion.58
  47.9 2.2 %fusion.119 = (f32[8,16,256]{2,1,0:T(8,128)S(1)}, f32[5,8,16,256]{3,0,2,1:T(8,128)S(1)}) fusion(bf16[1,5,8,16,256]{4,3,2,1,0:T(8,128)(2,1)S(1)} %copy-done.3, f32[5,8,16,256]{3,0,2,1:T(8,128)S(1)} %fusion.94, f32[5,8,16,256]{3,0,2,1:T(8,128)S(1)} %convolution_bitcast_fusion.8, f32[5,8,16,256]{3,0,2,1:T(8,128)S(1)} %convolution_bitcast_fusion.9, ...), kind=kOutput, calls=%fused_computation.134 | convolution fusion | flops 12275712 | bytes 5914724 | tf_op jit(solution)/shard_map/ec,exyz->cxyz/dot_general | solution.py:34
  50.1 0.0 copy-start.5
  50.2 1.0 copy.39
  51.2 1.9 %collective-permute-start.8 = (f32[5,1,16,256]{3,0,2,1:T(8,128)S(1)}, f32[5,1,16,256]{3,0,2,1:T(8,128)S(1)}, u32[]{:S(2)}, u32[]{:S(2)}) collective-permute-start(f32[5,1,16,256]{3,0,2,1:T(8,128)S(1)} %get-tuple-element.15), channel_id=1, source_target_pairs={{4,0},{8,4},{12,8},{5,1},{9,5},{13,9},{6,2},{10,6},{14,10},{7,3},{... | collective-permute-start | bytes 245768 | tf_op jit(solution)/shard_map/ppermute | solution.py:19
  53.1 2.4 %collective-permute-start.9 = (f32[5,1,16,256]{3,0,2,1:T(8,128)S(1)}, f32[5,1,16,256]{3,0,2,1:T(8,128)S(1)}, u32[]{:S(2)}, u32[]{:S(2)}) collective-permute-start(f32[5,1,16,256]{3,0,2,1:T(8,128)S(1)} %get-tuple-element.14), channel_id=1, source_target_pairs={{0,4},{4,8},{8,12},{1,5},{5,9},{9,13},{2,6},{6,10},{10,14},{3,7},{... | collective-permute-start | bytes 245768 | tf_op jit(solution)/shard_map/ppermute | solution.py:16
  55.6 0.3 fusion.158
  55.8 0.2 fusion.120
  56.0 0.1 fusion.156
  56.1 0.1 mul.57
  56.2 41.7 %psum.7 = f32[4096]{0:T(1024)S(1)} all-reduce(f32[4096]{0:T(1024)S(1)} %mul.57), channel_id=1, replica_groups=mesh['cond'=2,'gx'=4,'yz'=4] {'cond','gx','yz'}, use_global_device_ids=true, to_apply=%region_3.4 | all-reduce | flops 4096 | bytes 32768 | tf_op jit(solution)/shard_map/psum | solution.py:94
  97.9 0.6 dynamic_slice.3
  98.5 2.4 %collective-permute-start.10 = (f32[5,10,1,256]{3,0,2,1:T(8,128)S(1)}, f32[5,10,1,256]{3,0,2,1:T(8,128)S(1)}, u32[]{:S(2)}, u32[]{:S(2)}) collective-permute-start(f32[5,10,1,256]{3,0,2,1:T(8,128)S(1)} %get-tuple-element.9), channel_id=1, source_target_pairs={{1,0},{2,1},{3,2},{5,4},{6,5},{7,6},{9,8},{10,9},{11,10},{13,12},{... | collective-permute-start | bytes 153608 | tf_op jit(solution)/shard_map/ppermute | solution.py:19
  101.0 3.6 %collective-permute-start.11 = (f32[5,10,1,256]{3,0,2,1:T(8,128)S(1)}, f32[5,10,1,256]{3,0,2,1:T(8,128)S(1)}, u32[]{:S(2)}, u32[]{:S(2)}) collective-permute-start(f32[5,10,1,256]{3,0,2,1:T(8,128)S(1)} %get-tuple-element.8), channel_id=1, source_target_pairs={{0,1},{1,2},{2,3},{4,5},{5,6},{6,7},{8,9},{9,10},{10,11},{12,13},{... | collective-permute-start | bytes 153608 | tf_op jit(solution)/shard_map/ppermute | solution.py:16
  104.6 1.1 convolution_bitcast_fusion
  105.7 1.6 %collective-permute-done.11 = f32[5,10,1,256]{3,0,2,1:T(8,128)S(1)} collective-permute-done((f32[5,10,1,256]{3,0,2,1:T(8,128)S(1)}, f32[5,10,1,256]{3,0,2,1:T(8,128)S(1)}, u32[]{:S(2)}, u32[]{:S(2)}) %collective-permute-start.11) | collective-permute-done | bytes 51232 | tf_op jit(solution)/shard_map/ppermute | solution.py:16
  107.3 0.6 select_maximum_fusion
  108.0 1.0 convolution_bitcast_fusion.6
  109.0 1.2 %convolution_bitcast_fusion.7 = f32[5,8,16,256]{3,0,2,1:T(8,128)S(1)} fusion(f32[5,10,18,258]{3,0,2,1:T(8,128)S(1)} %select_maximum_fusion, f32[1,1,5,5]{3,2,1,0:T(8,128)S(1)} %copy.81), kind=kOutput, calls=%fused_computation.82 | convolution fusion | flops 9830400 | bytes 1708032 | tf_op jit(solution)/shard_map/ec,exyz->cxyz/dot_general | solution.py:34
  110.3 1.1 fusion.49
  111.3 1.1 fusion.52
  112.4 2.0 %fusion.86 = f32[1,5,8,16,256]{4,1,3,2,0:T(8,128)S(1)} fusion(f32[5,8,16,256]{3,0,2,1:T(8,128)S(1)} %convolution_bitcast_fusion.6, f32[5,8,16,256]{3,0,2,1:T(8,128)S(1)} %convolution_bitcast_fusion.7, f32[5,8,16,256]{3,0,2,1:T(8,128)S(1)} %fusion.49, f32[5,8,16,256]{3,0,2,1:T(8,128)S(1)} %fusion.52, f32[5,8,16,256]{3,0,2,1:T(8,128)S(1)} %convolution_bitcast_fusion, ...), kind=kOutput, calls=%fused_computation.100 | convolution fusion | flops 11325440 | bytes 5455972 | tf_op jit(solution)/shard_map/ec,exyz->cxyz/dot_general | solution.py:34
  114.4 1.0 copy.40
  (23 shorter events, 0.2 us)
Async XLA Ops:
  0.6 54.9 %copy-start = (f32[256,128]{1,0:T(8,128)S(1)}, f32[256,128]{1,0:T(8,128)}, u32[]{:S(2)}) copy-start(f32[256,128]{1,0:T(8,128)} %param.16) | copy-start | bytes 393220
  0.6 5.9 %copy-start.4 = (f32[1,6,5,5]{1,0,3,2:T(1,128)S(1)}, f32[1,6,5,5]{1,0,3,2:T(1,128)}, u32[]{:S(2)}) copy-start(f32[1,6,5,5]{1,0,3,2:T(1,128)} %param.12) | copy-start | bytes 1804
  0.7 6.9 %copy-start.6 = (s32[8,16]{1,0:T(8,128)S(1)}, s32[8,16]{1,0:T(8,128)}, u32[]{:S(2)}) copy-start(s32[8,16]{1,0:T(8,128)} %param.15) | copy-start | bytes 1540
  2.2 5.4 %collective-permute-start = (f32[5,1,16,256]{3,0,2,1:T(8,128)S(1)}, f32[5,1,16,256]{3,0,2,1:T(8,128)S(1)}, u32[]{:S(2)}, u32[]{:S(2)}) collective-permute-start(f32[5,1,16,256]{3,0,2,1:T(8,128)S(1)} %get-tuple-element.19), channel_id=1, source_target_pairs={{4,0},{8,4},{12,8},{5,1},{9,5},{13,9},{6,2},{10,6},{14,10},{7,3},{... | collective-permute-start | bytes 245768 | tf_op jit(solution)/shard_map/ppermute | solution.py:19
  4.1 6.3 %collective-permute-start.1 = (f32[5,1,16,256]{3,0,2,1:T(8,128)S(1)}, f32[5,1,16,256]{3,0,2,1:T(8,128)S(1)}, u32[]{:S(2)}, u32[]{:S(2)}) collective-permute-start(f32[5,1,16,256]{3,0,2,1:T(8,128)S(1)} %get-tuple-element.18), channel_id=1, source_target_pairs={{0,4},{4,8},{8,12},{1,5},{5,9},{9,13},{2,6},{6,10},{10,14},{3,7},{... | collective-permute-start | bytes 245768 | tf_op jit(solution)/shard_map/ppermute | solution.py:16
  10.4 6.9 %collective-permute-start.2 = (f32[5,10,1,256]{3,0,2,1:T(8,128)S(1)}, f32[5,10,1,256]{3,0,2,1:T(8,128)S(1)}, u32[]{:S(2)}, u32[]{:S(2)}) collective-permute-start(f32[5,10,1,256]{3,0,2,1:T(8,128)S(1)} %get-tuple-element.13), channel_id=1, source_target_pairs={{1,0},{2,1},{3,2},{5,4},{6,5},{7,6},{9,8},{10,9},{11,10},{13,12},{... | collective-permute-start | bytes 153608 | tf_op jit(solution)/shard_map/ppermute | solution.py:19
  12.8 6.3 %collective-permute-start.3 = (f32[5,10,1,256]{3,0,2,1:T(8,128)S(1)}, f32[5,10,1,256]{3,0,2,1:T(8,128)S(1)}, u32[]{:S(2)}, u32[]{:S(2)}) collective-permute-start(f32[5,10,1,256]{3,0,2,1:T(8,128)S(1)} %get-tuple-element.12), channel_id=1, source_target_pairs={{0,1},{1,2},{2,3},{4,5},{5,6},{6,7},{8,9},{9,10},{10,11},{12,13},{... | collective-permute-start | bytes 153608 | tf_op jit(solution)/shard_map/ppermute | solution.py:16
  22.1 2.2 %copy-start.1 = (f32[1,5,8,16,256]{4,3,2,1,0:T(8,128)S(1)}, f32[1,5,8,16,256]{4,3,2,1,0:T(8,128)}, u32[]{:S(2)}) copy-start(f32[1,5,8,16,256]{4,3,2,1,0:T(8,128)} %param.10) | copy-start | bytes 1966084
  22.1 2.2 %copy-start.2 = (f32[8,16,256]{2,1,0:T(8,128)S(1)}, f32[8,16,256]{2,1,0:T(8,128)}, u32[]{:S(2)}) copy-start(f32[8,16,256]{2,1,0:T(8,128)} %param.11) | copy-start | bytes 393220
  24.3 6.4 %copy-start.7 = (s32[2]{0:T(128)S(1)}, s32[2]{0:T(128)}, u32[]{:S(2)}) copy-start(s32[2]{0:T(128)} %param.17) | copy-start | bytes 28
  26.3 6.3 %collective-permute-start.4 = (f32[5,1,16,256]{3,0,2,1:T(8,128)S(1)}, f32[5,1,16,256]{3,0,2,1:T(8,128)S(1)}, u32[]{:S(2)}, u32[]{:S(2)}) collective-permute-start(f32[5,1,16,256]{3,0,2,1:T(8,128)S(1)} %get-tuple-element.17), channel_id=1, source_target_pairs={{4,0},{8,4},{12,8},{5,1},{9,5},{13,9},{6,2},{10,6},{14,10},{7,3},{... | collective-permute-start | bytes 245768 | tf_op jit(solution)/shard_map/ppermute | solution.py:19
  28.3 6.3 %collective-permute-start.5 = (f32[5,1,16,256]{3,0,2,1:T(8,128)S(1)}, f32[5,1,16,256]{3,0,2,1:T(8,128)S(1)}, u32[]{:S(2)}, u32[]{:S(2)}) collective-permute-start(f32[5,1,16,256]{3,0,2,1:T(8,128)S(1)} %get-tuple-element.16), channel_id=1, source_target_pairs={{0,4},{4,8},{8,12},{1,5},{5,9},{9,13},{2,6},{6,10},{10,14},{3,7},{... | collective-permute-start | bytes 245768 | tf_op jit(solution)/shard_map/ppermute | solution.py:16
  34.6 7.1 %collective-permute-start.6 = (f32[5,10,1,256]{3,0,2,1:T(8,128)S(1)}, f32[5,10,1,256]{3,0,2,1:T(8,128)S(1)}, u32[]{:S(2)}, u32[]{:S(2)}) collective-permute-start(f32[5,10,1,256]{3,0,2,1:T(8,128)S(1)} %get-tuple-element.11), channel_id=1, source_target_pairs={{1,0},{2,1},{3,2},{5,4},{6,5},{7,6},{9,8},{10,9},{11,10},{13,12},{... | collective-permute-start | bytes 153608 | tf_op jit(solution)/shard_map/ppermute | solution.py:19
  36.5 6.3 %collective-permute-start.7 = (f32[5,10,1,256]{3,0,2,1:T(8,128)S(1)}, f32[5,10,1,256]{3,0,2,1:T(8,128)S(1)}, u32[]{:S(2)}, u32[]{:S(2)}) collective-permute-start(f32[5,10,1,256]{3,0,2,1:T(8,128)S(1)} %get-tuple-element.10), channel_id=1, source_target_pairs={{0,1},{1,2},{2,3},{4,5},{5,6},{6,7},{8,9},{9,10},{10,11},{12,13},{... | collective-permute-start | bytes 153608 | tf_op jit(solution)/shard_map/ppermute | solution.py:16
  45.8 2.2 %copy-start.3 = (bf16[1,5,8,16,256]{4,3,2,1,0:T(8,128)(2,1)S(1)}, bf16[1,5,8,16,256]{4,3,2,1,0:T(8,128)(2,1)}, u32[]{:S(2)}) copy-start(bf16[1,5,8,16,256]{4,3,2,1,0:T(8,128)(2,1)} %param.13) | copy-start | bytes 983044
  50.1 5.4 %copy-start.5 = (s32[8,16,256]{2,1,0:T(8,128)S(1)}, s32[8,16,256]{2,1,0:T(8,128)}, u32[]{:S(2)}) copy-start(s32[8,16,256]{2,1,0:T(8,128)} %param.14) | copy-start | bytes 393220
  51.2 47.3 %collective-permute-start.8 = (f32[5,1,16,256]{3,0,2,1:T(8,128)S(1)}, f32[5,1,16,256]{3,0,2,1:T(8,128)S(1)}, u32[]{:S(2)}, u32[]{:S(2)}) collective-permute-start(f32[5,1,16,256]{3,0,2,1:T(8,128)S(1)} %get-tuple-element.15), channel_id=1, source_target_pairs={{4,0},{8,4},{12,8},{5,1},{9,5},{13,9},{6,2},{10,6},{14,10},{7,3},{... | collective-permute-start | bytes 245768 | tf_op jit(solution)/shard_map/ppermute | solution.py:19
  53.1 45.4 %collective-permute-start.9 = (f32[5,1,16,256]{3,0,2,1:T(8,128)S(1)}, f32[5,1,16,256]{3,0,2,1:T(8,128)S(1)}, u32[]{:S(2)}, u32[]{:S(2)}) collective-permute-start(f32[5,1,16,256]{3,0,2,1:T(8,128)S(1)} %get-tuple-element.14), channel_id=1, source_target_pairs={{0,4},{4,8},{8,12},{1,5},{5,9},{9,13},{2,6},{6,10},{10,14},{3,7},{... | collective-permute-start | bytes 245768 | tf_op jit(solution)/shard_map/ppermute | solution.py:16
  98.5 7.2 %collective-permute-start.10 = (f32[5,10,1,256]{3,0,2,1:T(8,128)S(1)}, f32[5,10,1,256]{3,0,2,1:T(8,128)S(1)}, u32[]{:S(2)}, u32[]{:S(2)}) collective-permute-start(f32[5,10,1,256]{3,0,2,1:T(8,128)S(1)} %get-tuple-element.9), channel_id=1, source_target_pairs={{1,0},{2,1},{3,2},{5,4},{6,5},{7,6},{9,8},{10,9},{11,10},{13,12},{... | collective-permute-start | bytes 153608 | tf_op jit(solution)/shard_map/ppermute | solution.py:19
  101.0 6.3 %collective-permute-start.11 = (f32[5,10,1,256]{3,0,2,1:T(8,128)S(1)}, f32[5,10,1,256]{3,0,2,1:T(8,128)S(1)}, u32[]{:S(2)}, u32[]{:S(2)}) collective-permute-start(f32[5,10,1,256]{3,0,2,1:T(8,128)S(1)} %get-tuple-element.8), channel_id=1, source_target_pairs={{0,1},{1,2},{2,3},{4,5},{5,6},{6,7},{8,9},{9,10},{10,11},{12,13},{... | collective-permute-start | bytes 153608 | tf_op jit(solution)/shard_map/ppermute | solution.py:16
where the time goes:
time: 116 us; the launch traced here: 115 us
  blocking collectives  41.7 us (36%)
  starting transfers between devices  30.9 us (27%)
  matrix products  23 us (20%)
  waiting for transfers between devices  9.19 us (8%)
  local copies, waits for them, and re-layouts  5.56 us (5%)
  other arithmetic  2.64 us (2%)
  between operations  2.47 us (2%)
    psum x1, blocking collectives, local(): summed = lax.psum(local_portion * gradient, ('cond', 'gx', 'yz'))  41.7 us
    dot_general x18, matrix products, apply_operator(): jnp.einsum('ec,exyz->cxyz', blocks[direction], shifted, precision=lax.Pre...  22.6 us
    ppermute x6, starting transfers between devices, with_halo(): lax.ppermute(lax.slice_in_dim(block, block.shape[dim] - width, None, axis...  18.4 us
    ppermute x6, starting transfers between devices, with_halo(): lax.ppermute(lax.slice_in_dim(block, 0, width, axis=dim), axis, backward)  12.5 us
    ppermute x6, waiting for transfers between devices, with_halo(): lax.ppermute(lax.slice_in_dim(block, block.shape[dim] - width, None, axis...  9.18 us
    unnamed x25, local copies, waits for them, and re-layouts  4.43 us
  transfers between devices with their start and end apart: 12, of which 5 were waited for; matrix products, arithmetic and copies ran while one was open for 5% of the time, Pallas kernels for 0%

commit v1 on v0

--- a/solution.py
+++ b/solution.py
@@ -91,7 +91,7 @@
     weights_float = condition_weights.astype(jnp.float32)
     picked = jnp.arange(weights_float.shape[0]) == lax.axis_index("cond")
     local_portion = jnp.sum(jnp.where(picked, weights_float, 0.0)) / jnp.sum(weights_float)
-    summed = lax.psum(local_portion * gradient, ("cond", "gx", "yz"))
+    summed = lax.psum(lax.psum(local_portion * gradient, ("gx", "yz")), "cond")
     pieces = NDES // lax.axis_size(("gx", "yz"))
     design_gradient = lax.dynamic_slice_in_dim(
         summed, lax.axis_index(("gx", "yz")) * pieces, pieces, 0

time: 116 us -> 145 us (1.25)
  blocking collectives: 41.7 us -> 67.1 us
  starting transfers between devices: 30.9 us -> 33 us
  waiting for transfers between devices: 9.19 us -> 10.7 us
    psum x1 -> x2, blocking collectives: 41.7 us -> 67.1 us  [local(): summed = lax.psum(lax.psum(local_portion * gradient, ('gx', 'yz')), 'cond')]
    ppermute x6, starting transfers between devices: 12.5 us -> 16 us  [with_halo(): lax.ppermute(lax.slice_in_dim(block, 0, width, axis=dim), axis, backward)]
    ppermute x6, starting transfers between devices: 18.4 us -> 17 us  [with_halo(): lax.ppermute(lax.slice_in_dim(block, block.shape[dim] - width, None, axis...]
    ppermute x6, waiting for transfers between devices: 9.18 us -> 10.7 us  [with_halo(): lax.ppermute(lax.slice_in_dim(block, block.shape[dim] - width, None, axis...]
  transfers between devices with their start and end apart: 12 -> 12, of which waited for: 5 -> 5; matrix products, arithmetic and copies ran while one was open for 5% -> 4% of each run, Pallas kernels for 0% -> 0%
where the time goes in v1:
time: 145 us; the launch traced here: 144 us
  blocking collectives  67.1 us (46%)
  starting transfers between devices  33 us (23%)
  matrix products  23 us (16%)
  waiting for transfers between devices  10.7 us (7%)
  local copies, waits for them, and re-layouts  5.55 us (4%)
  other arithmetic  2.64 us (2%)
  between operations  2.46 us (2%)
    psum x2, blocking collectives, local(): summed = lax.psum(lax.psum(local_portion * gradient, ('gx', 'yz')), 'cond')  67.1 us
    dot_general x18, matrix products, apply_operator(): jnp.einsum('ec,exyz->cxyz', blocks[direction], shifted, precision=lax.Pre...  22.6 us
    ppermute x6, starting transfers between devices, with_halo(): lax.ppermute(lax.slice_in_dim(block, block.shape[dim] - width, None, axis...  17 us
    ppermute x6, starting transfers between devices, with_halo(): lax.ppermute(lax.slice_in_dim(block, 0, width, axis=dim), axis, backward)  16 us
    ppermute x6, waiting for transfers between devices, with_halo(): lax.ppermute(lax.slice_in_dim(block, block.shape[dim] - width, None, axis...  10.7 us
    unnamed x25, local copies, waits for them, and re-layouts  4.43 us
  transfers between devices with their start and end apart: 12, of which 5 were waited for; matrix products, arithmetic and copies ran while one was open for 4% of the time, Pallas kernels for 0%

profile of v1, /device:TPU:12, one launch (start us, length us, event | category | flops | bytes accessed | tf_op | source)
XLA Modules:
  0.0 144.4 jit_solution(2325376474875346467)
XLA Ops:
  0.6 0.0 copy-start
  0.7 1.5 %copy.88 = f32[1,5,8,16,256]{4,1,3,2,0:T(8,128)S(1)} copy(f32[1,5,8,16,256]{4,3,2,1,0:T(8,128)} %param.9) | data formatting | bytes 1310720 | tf_op args[0]
  2.2 1.9 %collective-permute-start = (f32[5,1,16,256]{3,0,2,1:T(8,128)S(1)}, f32[5,1,16,256]{3,0,2,1:T(8,128)S(1)}, u32[]{:S(2)}, u32[]{:S(2)}) collective-permute-start(f32[5,1,16,256]{3,0,2,1:T(8,128)S(1)} %get-tuple-element.19), channel_id=1, source_target_pairs={{4,0},{8,4},{12,8},{5,1},{9,5},{13,9},{6,2},{10,6},{14,10},{7,3},{... | collective-permute-start | bytes 245768 | tf_op jit(solution)/shard_map/ppermute | solution.py:19
  4.1 2.4 %collective-permute-start.1 = (f32[5,1,16,256]{3,0,2,1:T(8,128)S(1)}, f32[5,1,16,256]{3,0,2,1:T(8,128)S(1)}, u32[]{:S(2)}, u32[]{:S(2)}) collective-permute-start(f32[5,1,16,256]{3,0,2,1:T(8,128)S(1)} %get-tuple-element.18), channel_id=1, source_target_pairs={{0,4},{4,8},{8,12},{1,5},{5,9},{9,13},{2,6},{6,10},{10,14},{3,7},{... | collective-permute-start | bytes 245768 | tf_op jit(solution)/shard_map/ppermute | solution.py:16
  6.6 0.2 fusion.157
  6.8 0.1 copy.82
  6.9 0.1 copy.81
  7.0 0.1 copy.80
  7.2 0.1 copy.79
  7.3 0.1 copy.78
  7.4 0.1 copy.77
  7.6 0.1 eq.24
  7.6 0.0 collective-permute-done
  7.7 2.8 %collective-permute-done.1 = f32[5,1,16,256]{3,0,2,1:T(8,128)S(1)} collective-permute-done((f32[5,1,16,256]{3,0,2,1:T(8,128)S(1)}, f32[5,1,16,256]{3,0,2,1:T(8,128)S(1)}, u32[]{:S(2)}, u32[]{:S(2)}) %collective-permute-start.1) | collective-permute-done | bytes 81952 | tf_op jit(solution)/shard_map/ppermute | solution.py:16
  10.4 2.4 %collective-permute-start.2 = (f32[5,10,1,256]{3,0,2,1:T(8,128)S(1)}, f32[5,10,1,256]{3,0,2,1:T(8,128)S(1)}, u32[]{:S(2)}, u32[]{:S(2)}) collective-permute-start(f32[5,10,1,256]{3,0,2,1:T(8,128)S(1)} %get-tuple-element.13), channel_id=1, source_target_pairs={{1,0},{2,1},{3,2},{5,4},{6,5},{7,6},{9,8},{10,9},{11,10},{13,12},{... | collective-permute-start | bytes 153608 | tf_op jit(solution)/shard_map/ppermute | solution.py:19
  12.8 3.5 %collective-permute-start.3 = (f32[5,10,1,256]{3,0,2,1:T(8,128)S(1)}, f32[5,10,1,256]{3,0,2,1:T(8,128)S(1)}, u32[]{:S(2)}, u32[]{:S(2)}) collective-permute-start(f32[5,10,1,256]{3,0,2,1:T(8,128)S(1)} %get-tuple-element.12), channel_id=1, source_target_pairs={{0,1},{1,2},{2,3},{4,5},{5,6},{6,7},{8,9},{9,10},{10,11},{12,13},{... | collective-permute-start | bytes 153608 | tf_op jit(solution)/shard_map/ppermute | solution.py:16
  16.3 1.1 convolution_bitcast_fusion.4
  17.4 1.8 %collective-permute-done.3 = f32[5,10,1,256]{3,0,2,1:T(8,128)S(1)} collective-permute-done((f32[5,10,1,256]{3,0,2,1:T(8,128)S(1)}, f32[5,10,1,256]{3,0,2,1:T(8,128)S(1)}, u32[]{:S(2)}, u32[]{:S(2)}) %collective-permute-start.3) | collective-permute-done | bytes 51232 | tf_op jit(solution)/shard_map/ppermute | solution.py:16
  19.1 0.6 select_maximum_fusion.8
  19.8 1.0 convolution_bitcast_fusion.10
  20.9 1.2 convolution_bitcast_fusion.11
  22.1 0.0 copy-start.1
  22.1 0.0 copy-start.2
  22.1 1.1 fusion.61
  23.2 1.1 fusion.64
  24.3 0.0 copy-start.7
  24.3 2.0 %fusion.94 = f32[5,8,16,256]{3,0,2,1:T(8,128)S(1)} fusion(f32[5,8,16,256]{3,0,2,1:T(8,128)S(1)} %bitcast.184, f32[5,8,16,256]{3,0,2,1:T(8,128)S(1)} %convolution_bitcast_fusion.10, f32[5,8,16,256]{3,0,2,1:T(8,128)S(1)} %convolution_bitcast_fusion.11, f32[5,8,16,256]{3,0,2,1:T(8,128)S(1)} %fusion.61, f32[5,8,16,256]{3,0,2,1:T(8,128)S(1)} %fusion.64, ...), kind=kOutput, calls=%fused_computation.108 | convolution fusion | flops 11816960 | bytes 5455972 | tf_op jit(solution)/shard_map/ec,exyz->cxyz/dot_general | solution.py:34
  26.3 1.9 %collective-permute-start.4 = (f32[5,1,16,256]{3,0,2,1:T(8,128)S(1)}, f32[5,1,16,256]{3,0,2,1:T(8,128)S(1)}, u32[]{:S(2)}, u32[]{:S(2)}) collective-permute-start(f32[5,1,16,256]{3,0,2,1:T(8,128)S(1)} %get-tuple-element.17), channel_id=1, source_target_pairs={{4,0},{8,4},{12,8},{5,1},{9,5},{13,9},{6,2},{10,6},{14,10},{7,3},{... | collective-permute-start | bytes 245768 | tf_op jit(solution)/shard_map/ppermute | solution.py:19
  28.3 2.4 %collective-permute-start.5 = (f32[5,1,16,256]{3,0,2,1:T(8,128)S(1)}, f32[5,1,16,256]{3,0,2,1:T(8,128)S(1)}, u32[]{:S(2)}, u32[]{:S(2)}) collective-permute-start(f32[5,1,16,256]{3,0,2,1:T(8,128)S(1)} %get-tuple-element.16), channel_id=1, source_target_pairs={{0,4},{4,8},{8,12},{1,5},{5,9},{9,13},{2,6},{6,10},{10,14},{3,7},{... | collective-permute-start | bytes 245768 | tf_op jit(solution)/shard_map/ppermute | solution.py:16
  30.7 0.6 convert_reduce_fusion
  32.7 1.9 %collective-permute-done.5 = f32[5,1,16,256]{3,0,2,1:T(8,128)S(1)} collective-permute-done((f32[5,1,16,256]{3,0,2,1:T(8,128)S(1)}, f32[5,1,16,256]{3,0,2,1:T(8,128)S(1)}, u32[]{:S(2)}, u32[]{:S(2)}) %collective-permute-start.5) | collective-permute-done | bytes 81952 | tf_op jit(solution)/shard_map/ppermute | solution.py:16
  34.6 1.9 %collective-permute-start.6 = (f32[5,10,1,256]{3,0,2,1:T(8,128)S(1)}, f32[5,10,1,256]{3,0,2,1:T(8,128)S(1)}, u32[]{:S(2)}, u32[]{:S(2)}) collective-permute-start(f32[5,10,1,256]{3,0,2,1:T(8,128)S(1)} %get-tuple-element.11), channel_id=1, source_target_pairs={{1,0},{2,1},{3,2},{5,4},{6,5},{7,6},{9,8},{10,9},{11,10},{13,12},{... | collective-permute-start | bytes 153608 | tf_op jit(solution)/shard_map/ppermute | solution.py:19
  36.5 4.1 %collective-permute-start.7 = (f32[5,10,1,256]{3,0,2,1:T(8,128)S(1)}, f32[5,10,1,256]{3,0,2,1:T(8,128)S(1)}, u32[]{:S(2)}, u32[]{:S(2)}) collective-permute-start(f32[5,10,1,256]{3,0,2,1:T(8,128)S(1)} %get-tuple-element.10), channel_id=1, source_target_pairs={{0,1},{1,2},{2,3},{4,5},{5,6},{6,7},{8,9},{9,10},{10,11},{12,13},{... | collective-permute-start | bytes 153608 | tf_op jit(solution)/shard_map/ppermute | solution.py:16
  40.6 1.1 convolution_bitcast_fusion.2
  41.7 1.1 collective-permute-done.7
  42.8 0.6 select_maximum_fusion.4
  43.5 1.0 convolution_bitcast_fusion.8
  44.5 1.2 convolution_bitcast_fusion.9
  45.8 0.0 copy-start.3
  45.8 1.1 fusion.55
  46.9 1.1 fusion.58
  47.9 2.2 %fusion.119 = (f32[8,16,256]{2,1,0:T(8,128)S(1)}, f32[5,8,16,256]{3,0,2,1:T(8,128)S(1)}) fusion(bf16[1,5,8,16,256]{4,3,2,1,0:T(8,128)(2,1)S(1)} %copy-done.3, f32[5,8,16,256]{3,0,2,1:T(8,128)S(1)} %fusion.94, f32[5,8,16,256]{3,0,2,1:T(8,128)S(1)} %convolution_bitcast_fusion.8, f32[5,8,16,256]{3,0,2,1:T(8,128)S(1)} %convolution_bitcast_fusion.9, ...), kind=kOutput, calls=%fused_computation.134 | convolution fusion | flops 12275712 | bytes 5914724 | tf_op jit(solution)/shard_map/ec,exyz->cxyz/dot_general | solution.py:34
  50.1 0.0 copy-start.5
  50.2 1.0 copy.39
  51.2 1.9 %collective-permute-start.8 = (f32[5,1,16,256]{3,0,2,1:T(8,128)S(1)}, f32[5,1,16,256]{3,0,2,1:T(8,128)S(1)}, u32[]{:S(2)}, u32[]{:S(2)}) collective-permute-start(f32[5,1,16,256]{3,0,2,1:T(8,128)S(1)} %get-tuple-element.15), channel_id=1, source_target_pairs={{4,0},{8,4},{12,8},{5,1},{9,5},{13,9},{6,2},{10,6},{14,10},{7,3},{... | collective-permute-start | bytes 245768 | tf_op jit(solution)/shard_map/ppermute | solution.py:19
  53.1 2.4 %collective-permute-start.9 = (f32[5,1,16,256]{3,0,2,1:T(8,128)S(1)}, f32[5,1,16,256]{3,0,2,1:T(8,128)S(1)}, u32[]{:S(2)}, u32[]{:S(2)}) collective-permute-start(f32[5,1,16,256]{3,0,2,1:T(8,128)S(1)} %get-tuple-element.14), channel_id=1, source_target_pairs={{0,4},{4,8},{8,12},{1,5},{5,9},{9,13},{2,6},{6,10},{10,14},{3,7},{... | collective-permute-start | bytes 245768 | tf_op jit(solution)/shard_map/ppermute | solution.py:16
  55.6 0.3 fusion.158
  55.8 0.2 fusion.120
  56.0 0.1 fusion.156
  56.1 0.1 mul.57
  56.2 58.9 %psum.14 = f32[4096]{0:T(1024)S(1)} all-reduce(f32[4096]{0:T(1024)S(1)} %mul.57), channel_id=1, replica_groups=mesh['cond'=2,'gx'=4,'yz'=4] {'gx','yz'}, use_global_device_ids=true, to_apply=%region_3.4 | all-reduce | flops 4096 | bytes 32768 | tf_op jit(solution)/shard_map/psum | solution.py:94
  115.1 8.1 %psum.15 = f32[4096]{0:T(1024)S(1)} all-reduce(f32[4096]{0:T(1024)S(1)} %psum.14), channel_id=1, replica_groups=mesh['cond'=2,'gx'=4,'yz'=4] {'cond'}, use_global_device_ids=true, to_apply=%region_4.5 | all-reduce | flops 4096 | bytes 32768 | tf_op jit(solution)/shard_map/psum | solution.py:94
  123.3 0.6 dynamic_slice.3
  123.9 6.0 %collective-permute-start.10 = (f32[5,10,1,256]{3,0,2,1:T(8,128)S(1)}, f32[5,10,1,256]{3,0,2,1:T(8,128)S(1)}, u32[]{:S(2)}, u32[]{:S(2)}) collective-permute-start(f32[5,10,1,256]{3,0,2,1:T(8,128)S(1)} %get-tuple-element.9), channel_id=1, source_target_pairs={{1,0},{2,1},{3,2},{5,4},{6,5},{7,6},{9,8},{10,9},{11,10},{13,12},{... | collective-permute-start | bytes 153608 | tf_op jit(solution)/shard_map/ppermute | solution.py:19
  129.9 2.1 %collective-permute-start.11 = (f32[5,10,1,256]{3,0,2,1:T(8,128)S(1)}, f32[5,10,1,256]{3,0,2,1:T(8,128)S(1)}, u32[]{:S(2)}, u32[]{:S(2)}) collective-permute-start(f32[5,10,1,256]{3,0,2,1:T(8,128)S(1)} %get-tuple-element.8), channel_id=1, source_target_pairs={{0,1},{1,2},{2,3},{4,5},{5,6},{6,7},{8,9},{9,10},{10,11},{12,13},{... | collective-permute-start | bytes 153608 | tf_op jit(solution)/shard_map/ppermute | solution.py:16
  132.1 1.1 convolution_bitcast_fusion
  133.2 3.1 %collective-permute-done.11 = f32[5,10,1,256]{3,0,2,1:T(8,128)S(1)} collective-permute-done((f32[5,10,1,256]{3,0,2,1:T(8,128)S(1)}, f32[5,10,1,256]{3,0,2,1:T(8,128)S(1)}, u32[]{:S(2)}, u32[]{:S(2)}) %collective-permute-start.11) | collective-permute-done | bytes 51232 | tf_op jit(solution)/shard_map/ppermute | solution.py:16
  136.3 0.6 select_maximum_fusion
  136.9 1.0 convolution_bitcast_fusion.6
  138.0 1.2 convolution_bitcast_fusion.7
  139.2 1.1 fusion.49
  140.3 1.1 fusion.52
  141.4 2.0 %fusion.86 = f32[1,5,8,16,256]{4,1,3,2,0:T(8,128)S(1)} fusion(f32[5,8,16,256]{3,0,2,1:T(8,128)S(1)} %convolution_bitcast_fusion.6, f32[5,8,16,256]{3,0,2,1:T(8,128)S(1)} %convolution_bitcast_fusion.7, f32[5,8,16,256]{3,0,2,1:T(8,128)S(1)} %fusion.49, f32[5,8,16,256]{3,0,2,1:T(8,128)S(1)} %fusion.52, f32[5,8,16,256]{3,0,2,1:T(8,128)S(1)} %convolution_bitcast_fusion, ...), kind=kOutput, calls=%fused_computation.100 | convolution fusion | flops 11325440 | bytes 5455972 | tf_op jit(solution)/shard_map/ec,exyz->cxyz/dot_general | solution.py:34
  143.4 1.0 copy.40
  (24 shorter events, 0.2 us)
Async XLA Ops:
  0.6 54.9 %copy-start = (f32[256,128]{1,0:T(8,128)S(1)}, f32[256,128]{1,0:T(8,128)}, u32[]{:S(2)}) copy-start(f32[256,128]{1,0:T(8,128)} %param.16) | copy-start | bytes 393220
  0.6 5.9 %copy-start.4 = (f32[1,6,5,5]{1,0,3,2:T(1,128)S(1)}, f32[1,6,5,5]{1,0,3,2:T(1,128)}, u32[]{:S(2)}) copy-start(f32[1,6,5,5]{1,0,3,2:T(1,128)} %param.12) | copy-start | bytes 1804
  0.7 6.9 %copy-start.6 = (s32[8,16]{1,0:T(8,128)S(1)}, s32[8,16]{1,0:T(8,128)}, u32[]{:S(2)}) copy-start(s32[8,16]{1,0:T(8,128)} %param.15) | copy-start | bytes 1540
  2.2 5.4 %collective-permute-start = (f32[5,1,16,256]{3,0,2,1:T(8,128)S(1)}, f32[5,1,16,256]{3,0,2,1:T(8,128)S(1)}, u32[]{:S(2)}, u32[]{:S(2)}) collective-permute-start(f32[5,1,16,256]{3,0,2,1:T(8,128)S(1)} %get-tuple-element.19), channel_id=1, source_target_pairs={{4,0},{8,4},{12,8},{5,1},{9,5},{13,9},{6,2},{10,6},{14,10},{7,3},{... | collective-permute-start | bytes 245768 | tf_op jit(solution)/shard_map/ppermute | solution.py:19
  4.1 6.3 %collective-permute-start.1 = (f32[5,1,16,256]{3,0,2,1:T(8,128)S(1)}, f32[5,1,16,256]{3,0,2,1:T(8,128)S(1)}, u32[]{:S(2)}, u32[]{:S(2)}) collective-permute-start(f32[5,1,16,256]{3,0,2,1:T(8,128)S(1)} %get-tuple-element.18), channel_id=1, source_target_pairs={{0,4},{4,8},{8,12},{1,5},{5,9},{9,13},{2,6},{6,10},{10,14},{3,7},{... | collective-permute-start | bytes 245768 | tf_op jit(solution)/shard_map/ppermute | solution.py:16
  10.4 6.9 %collective-permute-start.2 = (f32[5,10,1,256]{3,0,2,1:T(8,128)S(1)}, f32[5,10,1,256]{3,0,2,1:T(8,128)S(1)}, u32[]{:S(2)}, u32[]{:S(2)}) collective-permute-start(f32[5,10,1,256]{3,0,2,1:T(8,128)S(1)} %get-tuple-element.13), channel_id=1, source_target_pairs={{1,0},{2,1},{3,2},{5,4},{6,5},{7,6},{9,8},{10,9},{11,10},{13,12},{... | collective-permute-start | bytes 153608 | tf_op jit(solution)/shard_map/ppermute | solution.py:19
  12.8 6.3 %collective-permute-start.3 = (f32[5,10,1,256]{3,0,2,1:T(8,128)S(1)}, f32[5,10,1,256]{3,0,2,1:T(8,128)S(1)}, u32[]{:S(2)}, u32[]{:S(2)}) collective-permute-start(f32[5,10,1,256]{3,0,2,1:T(8,128)S(1)} %get-tuple-element.12), channel_id=1, source_target_pairs={{0,1},{1,2},{2,3},{4,5},{5,6},{6,7},{8,9},{9,10},{10,11},{12,13},{... | collective-permute-start | bytes 153608 | tf_op jit(solution)/shard_map/ppermute | solution.py:16
  22.1 2.2 %copy-start.1 = (f32[1,5,8,16,256]{4,3,2,1,0:T(8,128)S(1)}, f32[1,5,8,16,256]{4,3,2,1,0:T(8,128)}, u32[]{:S(2)}) copy-start(f32[1,5,8,16,256]{4,3,2,1,0:T(8,128)} %param.10) | copy-start | bytes 1966084
  22.1 2.2 %copy-start.2 = (f32[8,16,256]{2,1,0:T(8,128)S(1)}, f32[8,16,256]{2,1,0:T(8,128)}, u32[]{:S(2)}) copy-start(f32[8,16,256]{2,1,0:T(8,128)} %param.11) | copy-start | bytes 393220
  24.3 6.4 %copy-start.7 = (s32[2]{0:T(128)S(1)}, s32[2]{0:T(128)}, u32[]{:S(2)}) copy-start(s32[2]{0:T(128)} %param.17) | copy-start | bytes 28
  26.3 6.3 %collective-permute-start.4 = (f32[5,1,16,256]{3,0,2,1:T(8,128)S(1)}, f32[5,1,16,256]{3,0,2,1:T(8,128)S(1)}, u32[]{:S(2)}, u32[]{:S(2)}) collective-permute-start(f32[5,1,16,256]{3,0,2,1:T(8,128)S(1)} %get-tuple-element.17), channel_id=1, source_target_pairs={{4,0},{8,4},{12,8},{5,1},{9,5},{13,9},{6,2},{10,6},{14,10},{7,3},{... | collective-permute-start | bytes 245768 | tf_op jit(solution)/shard_map/ppermute | solution.py:19
  28.3 6.3 %collective-permute-start.5 = (f32[5,1,16,256]{3,0,2,1:T(8,128)S(1)}, f32[5,1,16,256]{3,0,2,1:T(8,128)S(1)}, u32[]{:S(2)}, u32[]{:S(2)}) collective-permute-start(f32[5,1,16,256]{3,0,2,1:T(8,128)S(1)} %get-tuple-element.16), channel_id=1, source_target_pairs={{0,4},{4,8},{8,12},{1,5},{5,9},{9,13},{2,6},{6,10},{10,14},{3,7},{... | collective-permute-start | bytes 245768 | tf_op jit(solution)/shard_map/ppermute | solution.py:16
  34.6 7.1 %collective-permute-start.6 = (f32[5,10,1,256]{3,0,2,1:T(8,128)S(1)}, f32[5,10,1,256]{3,0,2,1:T(8,128)S(1)}, u32[]{:S(2)}, u32[]{:S(2)}) collective-permute-start(f32[5,10,1,256]{3,0,2,1:T(8,128)S(1)} %get-tuple-element.11), channel_id=1, source_target_pairs={{1,0},{2,1},{3,2},{5,4},{6,5},{7,6},{9,8},{10,9},{11,10},{13,12},{... | collective-permute-start | bytes 153608 | tf_op jit(solution)/shard_map/ppermute | solution.py:19
  36.5 6.3 %collective-permute-start.7 = (f32[5,10,1,256]{3,0,2,1:T(8,128)S(1)}, f32[5,10,1,256]{3,0,2,1:T(8,128)S(1)}, u32[]{:S(2)}, u32[]{:S(2)}) collective-permute-start(f32[5,10,1,256]{3,0,2,1:T(8,128)S(1)} %get-tuple-element.10), channel_id=1, source_target_pairs={{0,1},{1,2},{2,3},{4,5},{5,6},{6,7},{8,9},{9,10},{10,11},{12,13},{... | collective-permute-start | bytes 153608 | tf_op jit(solution)/shard_map/ppermute | solution.py:16
  45.8 2.2 %copy-start.3 = (bf16[1,5,8,16,256]{4,3,2,1,0:T(8,128)(2,1)S(1)}, bf16[1,5,8,16,256]{4,3,2,1,0:T(8,128)(2,1)}, u32[]{:S(2)}) copy-start(bf16[1,5,8,16,256]{4,3,2,1,0:T(8,128)(2,1)} %param.13) | copy-start | bytes 983044
  50.1 5.4 %copy-start.5 = (s32[8,16,256]{2,1,0:T(8,128)S(1)}, s32[8,16,256]{2,1,0:T(8,128)}, u32[]{:S(2)}) copy-start(s32[8,16,256]{2,1,0:T(8,128)} %param.14) | copy-start | bytes 393220
  51.2 72.7 %collective-permute-start.8 = (f32[5,1,16,256]{3,0,2,1:T(8,128)S(1)}, f32[5,1,16,256]{3,0,2,1:T(8,128)S(1)}, u32[]{:S(2)}, u32[]{:S(2)}) collective-permute-start(f32[5,1,16,256]{3,0,2,1:T(8,128)S(1)} %get-tuple-element.15), channel_id=1, source_target_pairs={{4,0},{8,4},{12,8},{5,1},{9,5},{13,9},{6,2},{10,6},{14,10},{7,3},{... | collective-permute-start | bytes 245768 | tf_op jit(solution)/shard_map/ppermute | solution.py:19
  53.1 70.8 %collective-permute-start.9 = (f32[5,1,16,256]{3,0,2,1:T(8,128)S(1)}, f32[5,1,16,256]{3,0,2,1:T(8,128)S(1)}, u32[]{:S(2)}, u32[]{:S(2)}) collective-permute-start(f32[5,1,16,256]{3,0,2,1:T(8,128)S(1)} %get-tuple-element.14), channel_id=1, source_target_pairs={{0,4},{4,8},{8,12},{1,5},{5,9},{9,13},{2,6},{6,10},{10,14},{3,7},{... | collective-permute-start | bytes 245768 | tf_op jit(solution)/shard_map/ppermute | solution.py:16
  123.9 9.3 %collective-permute-start.10 = (f32[5,10,1,256]{3,0,2,1:T(8,128)S(1)}, f32[5,10,1,256]{3,0,2,1:T(8,128)S(1)}, u32[]{:S(2)}, u32[]{:S(2)}) collective-permute-start(f32[5,10,1,256]{3,0,2,1:T(8,128)S(1)} %get-tuple-element.9), channel_id=1, source_target_pairs={{1,0},{2,1},{3,2},{5,4},{6,5},{7,6},{9,8},{10,9},{11,10},{13,12},{... | collective-permute-start | bytes 153608 | tf_op jit(solution)/shard_map/ppermute | solution.py:19
  129.9 6.3 %collective-permute-start.11 = (f32[5,10,1,256]{3,0,2,1:T(8,128)S(1)}, f32[5,10,1,256]{3,0,2,1:T(8,128)S(1)}, u32[]{:S(2)}, u32[]{:S(2)}) collective-permute-start(f32[5,10,1,256]{3,0,2,1:T(8,128)S(1)} %get-tuple-element.8), channel_id=1, source_target_pairs={{0,1},{1,2},{2,3},{4,5},{5,6},{6,7},{8,9},{9,10},{10,11},{12,13},{... | collective-permute-start | bytes 153608 | tf_op jit(solution)/shard_map/ppermute | solution.py:16
